TPU v7x, 32 devices: a whole 2x2x4 slice. The times are simulated.
32 devices in a mesh: grp: 2 (over y), blk: 16 (over z, x, core).
Axes of the slice: x: 2, y: 2, z: 4, core: 2. Of those that a mesh axis runs over, the one named last changes fastest.
Arguments:
- queries: bfloat16 [2048, 4096], P('blk'), may hold values from -15 to 15
- cache_keys: bfloat16 [1024, 512], P(('grp', 'blk')), may hold values from -5 to 5
- cache_values: bfloat16 [1024, 512], P(('grp', 'blk')), may hold values from -6 to 6
- new_keys: bfloat16 [2048, 512], P('blk'), may hold values from -6 to 6
- new_values: bfloat16 [2048, 512], P('blk'), may hold values from -6 to 6
- prefix_length: int32 [1], replicated, may hold values from 512 to 1024
- token_order: int32 [2048], P('blk'), may hold values from 0 to 2047, as said below
Outputs:
- attended: bfloat16 [2048, 4096], P('blk', 'grp')
Inputs may be any that keep to these rules, and one draw needn't show every extreme that they name: Cache slots from prefix_length[0] on are unused. `token_order`: a permutation of 0 to 2047 made of runs of 64 consecutive values, each run starting at a multiple of 64.
All inputs are finite; a program needn't handle non-finite values.
Results may differ from a plain program's by a relative error of at most 0.0044.
Values may be sent and summed in bfloat16 or wider, within the bound.
A program may use at most 64 MiB of HBM per device.

v0:
```python
import functools
import math

import jax
import jax.numpy as jnp
from jax import lax
from jax.experimental import pallas as pl
from jax.experimental.pallas import tpu as pltpu
from jax.sharding import PartitionSpec as P

HQ = 32
KVH = 4
HD = 128
MESH = pl.DeviceIdType.MESH
MASKED = -1e30
TILES = 1


def nearest_first(z_count):
    return [sorted(range(z_count), key=lambda other: (abs(other - z), abs(2 * other - z_count + 1))) for z in range(z_count)]


def pick(z, column):
    value = jnp.int32(column[0])
    for at in range(1, len(column)):
        value = jnp.where(z == at, jnp.int32(column[at]), value)
    return value


def kernel(
    groups, blocks,
    q_hbm, ck_hbm, cv_hbm, nk_hbm, nv_hbm, prefix_ref, order_hbm,
    out_ref,
    nbuf, cbuf, obuf, stage, qraw, qs, order_q, m_s, l_s, acc_s,
    load_sem, y_send, y_recv,
    up_send, down_send, x_send, sib_send, sibx_send,
    z_recv, x_recv, sib_recv, sibx_recv,
):
    heads = HQ // groups
    group_size = HQ // KVH
    kv_count = max(1, heads // group_size)
    sub_heads = heads // kv_count
    cols = kv_count * HD
    tok = nbuf.shape[1]
    slots = ck_hbm.shape[0]
    z_count = blocks // 4
    rows = sub_heads * tok

    g = lax.axis_index("grp")
    me = lax.axis_index("blk")
    z = me // 4
    x = (me // 2) % 2
    c = me % 2

    def block_of(zz, xx, cc):
        return (zz * 2 + xx) * 2 + cc

    sibling = block_of(z, x, 1 - c)
    across = block_of(z, 1 - x, c)
    has_up = z < z_count - 1
    has_down = z > 0
    middle = jnp.logical_and(has_up, has_down)

    def head_cols(group):
        return pl.ds(pl.multiple_of((group * heads // group_size) * HD, HD), cols)

    loads = [
        pltpu.make_async_copy(nk_hbm.at[:, head_cols(g)], nbuf.at[me, :, pl.ds(0, cols)], load_sem.at[0]),
        pltpu.make_async_copy(nv_hbm.at[:, head_cols(g)], nbuf.at[me, :, pl.ds(cols, cols)], load_sem.at[1]),
        pltpu.make_async_copy(order_hbm, obuf.at[me], load_sem.at[2]),
        pltpu.make_async_copy(ck_hbm, stage.at[0], load_sem.at[3]),
        pltpu.make_async_copy(cv_hbm, stage.at[1], load_sem.at[4]),
        pltpu.make_async_copy(ck_hbm.at[:, head_cols(g)], cbuf.at[me, pl.ds(g * slots, slots), pl.ds(0, cols)], load_sem.at[5]),
        pltpu.make_async_copy(cv_hbm.at[:, head_cols(g)], cbuf.at[me, pl.ds(g * slots, slots), pl.ds(cols, cols)], load_sem.at[6]),
        pltpu.make_async_copy(q_hbm.at[:, pl.ds(pl.multiple_of(g * heads * HD, HD), heads * HD)], qraw, load_sem.at[7]),
    ]
    for load in loads:
        load.start()

    barrier = pltpu.get_barrier_semaphore()

    def greet(group, block):
        pl.semaphore_signal(barrier, inc=1, device_id=(group, block), device_id_type=MESH)

    greet(g, sibling)
    greet(g, across)
    for step in range(1, groups):
        greet((g + step) % groups, me)
    pl.when(has_up)(lambda: greet(g, me + 4))
    pl.when(has_down)(lambda: greet(g, me - 4))
    pl.semaphore_wait(barrier, 1 + groups + jnp.where(has_up, 1, 0) + jnp.where(has_down, 1, 0))

    bufs = (nbuf, obuf, cbuf)

    def remote(kind, block, target, send, recv, at):
        ref = bufs[kind].at[block]
        return pltpu.make_async_remote_copy(
            src_ref=ref, dst_ref=ref, send_sem=send.at[kind, at], recv_sem=recv.at[kind, at],
            device_id=(g, target), device_id_type=MESH,
        )

    def send_up(kind, zz):
        return remote(kind, block_of(zz, x, c), me + 4, up_send, z_recv, zz)

    def send_down(kind, zz):
        return remote(kind, block_of(zz, x, c), me - 4, down_send, z_recv, zz)

    def send_x(kind, zz):
        return remote(kind, block_of(zz, x, c), across, x_send, x_recv, zz)

    def send_sib(kind, zz):
        return remote(kind, block_of(zz, x, c), sibling, sib_send, sib_recv, zz)

    def send_sibx(kind, zz):
        return remote(kind, block_of(zz, 1 - x, c), sibling, sibx_send, sibx_recv, zz)

    for load in loads[3:5]:
        load.wait()
    swaps = []
    for step in range(1, groups):
        other = (g + step) % groups
        for part in range(2):
            swaps.append(pltpu.make_async_remote_copy(
                src_ref=stage.at[part, :, head_cols(other)],
                dst_ref=cbuf.at[me, pl.ds(g * slots, slots), pl.ds(part * cols, cols)],
                send_sem=y_send.at[step, part], recv_sem=y_recv.at[step, part],
                device_id=(other, me), device_id_type=MESH,
            ))
    for swap in swaps:
        swap.start()

    def launch_own(kind):
        pl.when(has_up)(lambda: send_up(kind, z).start())
        pl.when(has_down)(lambda: send_down(kind, z).start())
        send_x(kind, z).start()
        send_sib(kind, z).start()

    for load in loads[:3]:
        load.wait()
    launch_own(0)
    launch_own(1)
    for load in loads[5:7]:
        load.wait()

    loads[7].wait()
    factor = HD ** -0.5 * math.log2(math.e)
    for head in range(heads):
        scaled = qraw[:, head * HD:(head + 1) * HD].astype(jnp.float32) * factor
        high = scaled.astype(jnp.bfloat16)
        low = (scaled - high.astype(jnp.float32)).astype(jnp.bfloat16)
        kv, sub = head // sub_heads, head % sub_heads
        qs[kv, sub * tok:(sub + 1) * tok, 0:HD] = high
        qs[kv, sub * tok:(sub + 1) * tok, HD:2 * HD] = low
    order_q[...] = jnp.broadcast_to(obuf[me].astype(jnp.float32), (tok, tok)).T

    for swap in swaps:
        swap.wait_recv()
    launch_own(2)

    prefix = prefix_ref[0]

    def attend(zz, xx, first=False):
        block = block_of(zz, xx, 0)
        cache_rows = cbuf.shape[1]
        lane = lax.broadcasted_iota(jnp.int32, (1, 2 * cache_rows), 1)
        within = lane % cache_rows
        slot = (within // slots) * (slots * blocks) + (block + lane // cache_rows) * slots + within % slots
        cache_bias = jnp.where(slot < prefix, 0.0, MASKED).astype(jnp.float32)
        pieces = [
            jnp.where(obuf[block + at].astype(jnp.float32) <= order_q[...], 0.0, MASKED) for at in range(2)
        ] + [jnp.broadcast_to(cache_bias, (tok, 2 * cache_rows))]
        bias = jnp.concatenate(pieces, axis=1)
        keys_n = 2 * (tok + cache_rows)
        rows = sub_heads * tok

        def gathered(at):
            return jnp.concatenate(
                [nbuf[block, :, at], nbuf[block + 1, :, at], cbuf[block, :, at], cbuf[block + 1, :, at]], axis=0
            )

        def operands(kv):
            keys = gathered(slice(kv * HD, (kv + 1) * HD))
            values = gathered(slice(cols + kv * HD, cols + (kv + 1) * HD))
            ones = jnp.ones((keys_n, HD), jnp.bfloat16)
            return jnp.concatenate([keys, keys], axis=1), jnp.concatenate([values, ones], axis=1)

        heads_tile = max(1, sub_heads // TILES)
        rows = heads_tile * tok
        pairs = [operands(kv) for kv in range(kv_count)]
        tiles = [(kv, sub) for kv in range(kv_count) for sub in range(0, sub_heads, heads_tile)]

        def score(kv, sub):
            at = slice(sub * tok, sub * tok + rows)
            return lax.dot_general(
                qs[kv, at], pairs[kv][0], (((1,), (1,)), ((), ())), preferred_element_type=jnp.float32
            )

        ahead = score(*tiles[0])
        for index, (kv, sub) in enumerate(tiles):
            s = ahead
            if index + 1 < len(tiles):
                ahead = score(*tiles[index + 1])
            at = slice(sub * tok, sub * tok + rows)
            s = (s.reshape(heads_tile, tok, keys_n) + bias[None]).reshape(rows, keys_n)
            chunks = [s[:, lanes:lanes + HD] for lanes in range(0, keys_n, HD)]
            peak = jnp.max(functools.reduce(jnp.maximum, chunks), axis=1, keepdims=True)
            if first:
                new_max = jnp.broadcast_to(peak, (rows, HD))
            else:
                old_max = m_s[kv, at]
                new_max = jnp.maximum(old_max, peak)
            p = jnp.concatenate([jnp.exp2(chunk - new_max).astype(jnp.bfloat16) for chunk in chunks], axis=1)
            o = jnp.dot(p, pairs[kv][1], preferred_element_type=jnp.float32)
            m_s[kv, at] = new_max
            if first:
                l_s[kv, at] = o[:, HD:]
                acc_s[kv, at] = o[:, :HD]
            else:
                alpha = jnp.exp2(old_max - new_max)
                l_s[kv, at] = l_s[kv, at] * alpha + o[:, HD:]
                acc_s[kv, at] = acc_s[kv, at] * alpha + o[:, :HD]

    def arrive_z(zz):
        for kind in range(3):
            remote(kind, block_of(zz, x, c), across, x_send, z_recv, zz).wait_recv()
            pl.when(jnp.logical_and(zz < z, has_up))(lambda: send_up(kind, zz).start())
            pl.when(jnp.logical_and(zz > z, has_down))(lambda: send_down(kind, zz).start())
            send_x(kind, zz).start()
            send_sib(kind, zz).start()

    def arrive_x(zz):
        for kind in range(3):
            remote(kind, block_of(zz, 1 - x, c), across, x_send, x_recv, zz).wait_recv()
            send_sibx(kind, zz).start()

    def own_column(zz, first=False):
        for kind in range(3):
            remote(kind, block_of(zz, x, 1 - c), sibling, sib_send, sib_recv, zz).wait_recv()
        attend(zz, x, first)

    def other_column(zz):
        for kind in range(3):
            remote(kind, block_of(zz, 1 - x, 1 - c), sibling, sibx_send, sibx_recv, zz).wait_recv()
        attend(zz, 1 - x)

    table = nearest_first(z_count)
    zs = [pick(z, [table[at][step] for at in range(z_count)]) for step in range(z_count)]

    own_column(z, first=True)
    for step in range(1, z_count):
        if step == 1:
            arrive_z(zs[1])
        else:
            pl.when(jnp.logical_not(middle))(lambda: arrive_z(zs[step]))
        if step + 1 < z_count:
            pl.when(middle)(lambda: arrive_z(zs[step + 1]))
        arrive_x(zs[step - 1])
        own_column(zs[step])
        other_column(zs[step - 1])
    last = zs[z_count - 1]
    arrive_x(last)
    other_column(last)

    for head in range(heads):
        kv, sub = head // sub_heads, head % sub_heads
        at = slice(sub * tok, (sub + 1) * tok)
        out_ref[:, head * HD:(head + 1) * HD] = (acc_s[kv, at] / l_s[kv, at]).astype(out_ref.dtype)

    for swap in swaps:
        swap.wait_send()
    for kind in range(3):
        pl.when(has_up)(lambda: send_up(kind, z).wait_send())
        pl.when(has_down)(lambda: send_down(kind, z).wait_send())
        for zz in range(z_count):
            pl.when(jnp.logical_and(zz < z, has_up))(lambda: send_up(kind, zz).wait_send())
            pl.when(jnp.logical_and(zz > z, has_down))(lambda: send_down(kind, zz).wait_send())
            send_x(kind, zz).wait_send()
            send_sib(kind, zz).wait_send()
            send_sibx(kind, zz).wait_send()


def solution(mesh):
    groups = mesh.shape["grp"]
    blocks = mesh.shape["blk"]

    def on_device(queries, cache_keys, cache_values, new_keys, new_values, prefix_length, token_order):
        tok = queries.shape[0]
        slots = cache_keys.shape[0]
        heads = HQ // groups
        kv_count = max(1, heads // (HQ // KVH))
        cols = kv_count * HD
        rows = heads // kv_count * tok
        z_count = blocks // 4
        dma = pltpu.SemaphoreType.DMA
        hbm = pl.BlockSpec(memory_space=pl.ANY)
        return pl.pallas_call(
            functools.partial(kernel, groups, blocks),
            out_shape=jax.ShapeDtypeStruct((tok, heads * HD), jnp.bfloat16),
            in_specs=[hbm] * 5 + [pl.BlockSpec(memory_space=pltpu.SMEM), hbm],
            out_specs=pl.BlockSpec(memory_space=pltpu.VMEM),
            scratch_shapes=[
                pltpu.VMEM((blocks, tok, 2 * cols), jnp.bfloat16),
                pltpu.VMEM((blocks, groups * slots, 2 * cols), jnp.bfloat16),
                pltpu.VMEM((blocks, 1, tok), jnp.int32),
                pltpu.VMEM((2, slots, KVH * HD), jnp.bfloat16),
                pltpu.VMEM((tok, heads * HD), jnp.bfloat16),
                pltpu.VMEM((kv_count, rows, 2 * HD), jnp.bfloat16),
                pltpu.VMEM((tok, tok), jnp.float32),
                pltpu.VMEM((kv_count, rows, HD), jnp.float32),
                pltpu.VMEM((kv_count, rows, HD), jnp.float32),
                pltpu.VMEM((kv_count, rows, HD), jnp.float32),
                dma((8,)), dma((groups, 2)), dma((groups, 2)),
                dma((3, z_count)), dma((3, z_count)), dma((3, z_count)), dma((3, z_count)), dma((3, z_count)),
                dma((3, z_count)), dma((3, z_count)), dma((3, z_count)), dma((3, z_count)),
            ],
            compiler_params=pltpu.CompilerParams(
                collective_id=0, has_side_effects=True, vmem_limit_bytes=60 * 1024 * 1024
            ),
        )(queries, cache_keys, cache_values, new_keys, new_values, prefix_length, token_order.reshape(1, tok))

    placed = (
        P("blk", None), P(("grp", "blk"), None), P(("grp", "blk"), None),
        P("blk", None), P("blk", None), P(), P("blk"),
    )
    return jax.shard_map(on_device, mesh=mesh, in_specs=placed, out_specs=P("blk", "grp"), check_vma=False)
```

profile of v0, /device:TPU:0, one launch (start us, length us, event | category | flops | bytes accessed | tf_op | source)
XLA Modules:
  0.0 32.6 jit_solution(10495304809325243894)
XLA Ops:
  0.7 30.0 %shard_map.73 = bf16[128,2048]{1,0:T(8,128)(2,1)} custom-call(bf16[128,4096]{1,0:T(8,128)(2,1)} %q_hbm.1, bf16[32,512]{1,0:T(8,128)(2,1)} %ck_hbm.1, bf16[32,512]{1,0:T(8,128)(2,1)} %cv_hbm.1, bf16[128,512]{1,0:T(8,128)(2,1)} %nk_hbm.1, bf16[128,512]{1,0:T(8,128)(2,1)} %nv_hbm.1, s32[1]{0:T(128)S(6)} %copy.9.prefix_ref, s32[1,128]{1,0:T(1,128)} %bitcast.1), custom_call_target="tpu_custom_call" | custom-call | tf_op jit(solution)/shard_map/pallas_call | solution.py:296
  30.7 1.9 %copy.10 = bf16[128,2048]{1,0:T(8,128)(2,1)} copy(bf16[128,2048]{1,0:T(8,128)(2,1)} %shard_map.73) | data formatting | bytes 1048576
where the time goes:
time: 32.7 us; the launch traced here: 32.6 us
  Pallas kernels  30 us (92%)
  local copies, waits for them, and re-layouts  1.88 us (6%)
  between operations  0.66 us (2%)
    pallas_call x1, Pallas kernels, on_device(): pl.pallas_call(functools.partial(kernel, groups, blocks), out_shape=jax.S...  30 us
    unnamed x1, local copies, waits for them, and re-layouts  1.88 us

commit v1 on v0

--- a/solution.py
+++ b/solution.py
@@ -15,17 +15,14 @@
 MASKED = -1e30
 TILES = 1
 
-
 def nearest_first(z_count):
     return [sorted(range(z_count), key=lambda other: (abs(other - z), abs(2 * other - z_count + 1))) for z in range(z_count)]
-
 
 def pick(z, column):
     value = jnp.int32(column[0])
     for at in range(1, len(column)):
         value = jnp.where(z == at, jnp.int32(column[at]), value)
     return value
-
 
 def kernel(
     groups, blocks,
@@ -74,6 +71,7 @@
         pltpu.make_async_copy(cv_hbm.at[:, head_cols(g)], cbuf.at[me, pl.ds(g * slots, slots), pl.ds(cols, cols)], load_sem.at[6]),
         pltpu.make_async_copy(q_hbm.at[:, pl.ds(pl.multiple_of(g * heads * HD, HD), heads * HD)], qraw, load_sem.at[7]),
     ]
+
     for load in loads:
         load.start()
 
@@ -278,6 +276,9 @@
             send_sib(kind, zz).wait_send()
             send_sibx(kind, zz).wait_send()
 
+def in_hbm(array):
+    return pltpu.with_memory_space_constraint(array, pltpu.HBM)
+
 
 def solution(mesh):
     groups = mesh.shape["grp"]
@@ -292,7 +293,7 @@
         rows = heads // kv_count * tok
         z_count = blocks // 4
         dma = pltpu.SemaphoreType.DMA
-        hbm = pl.BlockSpec(memory_space=pl.ANY)
+        hbm = pl.BlockSpec(memory_space=pltpu.HBM)
         return pl.pallas_call(
             functools.partial(kernel, groups, blocks),
             out_shape=jax.ShapeDtypeStruct((tok, heads * HD), jnp.bfloat16),
@@ -314,9 +315,12 @@
                 dma((3, z_count)), dma((3, z_count)), dma((3, z_count)), dma((3, z_count)),
             ],
             compiler_params=pltpu.CompilerParams(
-                collective_id=0, has_side_effects=True, vmem_limit_bytes=60 * 1024 * 1024
+                collective_id=0, has_side_effects=True, vmem_limit_bytes=28 * 1024 * 1024
             ),
-        )(queries, cache_keys, cache_values, new_keys, new_values, prefix_length, token_order.reshape(1, tok))
+        )(
+            *[in_hbm(a) for a in (queries, cache_keys, cache_values, new_keys, new_values)],
+            prefix_length, in_hbm(token_order.reshape(1, tok)),
+        )
 
     placed = (
         P("blk", None), P(("grp", "blk"), None), P(("grp", "blk"), None),

time: 32.7 us -> 30.8 us (0.942)
  local copies, waits for them, and re-layouts: 1.88 us -> 0.8 us
  Pallas kernels: 30 us -> 29.2 us
    unnamed x1, local copies, waits for them, and re-layouts: 1.88 us -> 0.8 us
    pallas_call x1, Pallas kernels: 30 us -> 29.2 us  [on_device(): pl.pallas_call(functools.partial(kernel, groups, blocks), out_shape=jax.S...]
where the time goes in v1:
time: 30.8 us; the launch traced here: 30.7 us
  Pallas kernels  29.2 us (95%)
  local copies, waits for them, and re-layouts  0.8 us (3%)
  between operations  0.66 us (2%)
    pallas_call x1, Pallas kernels, on_device(): pl.pallas_call(functools.partial(kernel, groups, blocks), out_shape=jax.S...  29.2 us
    unnamed x1, local copies, waits for them, and re-layouts  0.8 us

profile of v1, /device:TPU:0, one launch (start us, length us, event | category | flops | bytes accessed | tf_op | source)
XLA Modules:
  0.0 30.7 jit_solution(7986346327461815420)
XLA Ops:
  0.7 29.2 %shard_map.73 = bf16[128,2048]{1,0:T(8,128)(2,1)S(1)} custom-call(bf16[128,4096]{1,0:T(8,128)(2,1)} %q_hbm.1, bf16[32,512]{1,0:T(8,128)(2,1)} %ck_hbm.1, bf16[32,512]{1,0:T(8,128)(2,1)} %cv_hbm.1, bf16[128,512]{1,0:T(8,128)(2,1)} %nk_hbm.1, bf16[128,512]{1,0:T(8,128)(2,1)} %nv_hbm.1, s32[1]{0:T(128)S(6)} %copy.9.prefix_ref, s32[1,128]{1,0:T(1,128)} %bitcast.1), custom_call_target="tpu_custom_call" | custom-call | tf_op jit(solution)/shard_map/pallas_call | solution.py:297
  29.9 0.8 %copy.10 = bf16[128,2048]{1,0:T(8,128)(2,1)} copy(bf16[128,2048]{1,0:T(8,128)(2,1)S(1)} %shard_map.73) | data formatting | bytes 1048576
